TPU v7x, 32 devices: a whole 2x2x4 slice. The times are simulated.
32 devices in a mesh: gx: 4 (over z), gy: 4 (over x, core), gz: 2 (over y).
Axes of the slice: x: 2, y: 2, z: 4, core: 2. Of those that a mesh axis runs over, the one named last changes fastest.
Arguments:
- pair: bfloat16 [1024, 1024, 128], P('gx', 'gy'), may hold values from -8 to 8, as said below
- residue_mask: int32 [1024], replicated, may hold values 0 or 1
- ln_in_gain: float32 [128], replicated, may hold values from 0.1 to 1.9
- w_proj: bfloat16 [128, 4, 128], P(None, None, 'gz'), may hold values from -0.5 to 0.5
- w_gate: bfloat16 [128, 128], replicated, may hold values from -0.5 to 0.5
- ln_out_gain: float32 [128], replicated, may hold values from 0.1 to 1.9
- w_out: bfloat16 [128, 128], replicated, may hold values from -0.5 to 0.5
Outputs:
- update: bfloat16 [128, 1024, 1024], P(None, ('gx', 'gz'), 'gy')
- energy: float32 [], replicated
Inputs may be any that keep to these rules, and one draw needn't show every extreme that they name: pair is symmetric in its two residue indices: pair[i, j, c] equals pair[j, i, c].
All inputs are finite; a program needn't handle non-finite values.
Results may differ from a plain program's by a relative error of at most 0.0083.
Values may be sent and summed in bfloat16 or wider, within the bound.
A program may use at most 256 MiB of HBM per device.

v0:
```python
import jax
import jax.numpy as jnp
from jax import lax
from jax.sharding import PartitionSpec as P

NORM_EPS = 1e-05


def layer_norm(values, gain_vec, axis):
    mean_val = jnp.mean(values, axis=axis, keepdims=True)
    centred = values - mean_val
    variance = jnp.mean(centred * centred, axis=axis, keepdims=True)
    return centred * lax.rsqrt(variance + NORM_EPS) * gain_vec


def batched(first, second):
    return jnp.einsum("hik,hkj->hij", first, second, preferred_element_type=jnp.float32)


def local(pair, residue_mask, ln_in_gain, w_proj, w_gate, ln_out_gain, w_out):
    tile_len = pair.shape[0]
    channel_count = pair.shape[2]
    grid_len = lax.axis_size("gx")
    slab_count = lax.axis_size("gz")
    slab_rows = tile_len // slab_count
    total_len = tile_len * grid_len
    row_block = lax.axis_index("gx")
    col_block = lax.axis_index("gy")
    slab_index = lax.axis_index("gz")
    mask_float = residue_mask.astype(jnp.float32)
    row_mask = lax.dynamic_slice_in_dim(mask_float, row_block * tile_len, tile_len)
    col_mask = lax.dynamic_slice_in_dim(mask_float, col_block * tile_len, tile_len)
    tile_mask = row_mask[:, None] * col_mask[None, :]
    normed = layer_norm(pair.astype(jnp.float32), ln_in_gain, -1).astype(jnp.bfloat16)
    projected = jnp.einsum("ijd,dkh->khij", normed, w_proj, preferred_element_type=jnp.float32)
    left_tile = (tile_mask * jax.nn.sigmoid(projected[0]) * projected[1]).astype(jnp.bfloat16)
    right_tile = (tile_mask * jax.nn.sigmoid(projected[2]) * projected[3]).astype(jnp.bfloat16)
    col_left, col_right = (
        lax.all_gather(left_tile, "gx", axis=1, tiled=True),
        lax.all_gather(right_tile, "gx", axis=1, tiled=True),
    )
    piece_left = lax.all_gather(left_tile, "gy", axis=2, tiled=True)
    piece_right = lax.all_gather(right_tile, "gy", axis=2, tiled=True)
    below_left = col_left
    below_right = col_right
    below_left, below_right = (below_left, below_right)
    summed = batched(piece_left, below_right) + batched(piece_right, below_left)
    tri_map = (0.5 * summed).astype(jnp.bfloat16)
    tri_normed = layer_norm(
        lax.all_to_all(tri_map, "gz", split_axis=1, concat_axis=0, tiled=True).astype(jnp.float32),
        ln_out_gain[:, None, None],
        0,
    ).astype(jnp.bfloat16)
    mixed = jnp.einsum("hij,hc->cij", tri_normed, w_out, preferred_element_type=jnp.float32)
    slab_normed = lax.dynamic_slice_in_dim(normed, slab_index * slab_rows, slab_rows, 0)
    gate_vals = jax.nn.sigmoid(
        jnp.einsum("ijd,dc->cij", slab_normed, w_gate, preferred_element_type=jnp.float32)
    )
    update = (gate_vals * mixed).astype(jnp.bfloat16)
    row_start = row_block * tile_len + slab_index * slab_rows
    row_float = (row_start + jnp.arange(slab_rows, dtype=jnp.int32)).astype(jnp.float32)
    col_float = (col_block * tile_len + jnp.arange(tile_len, dtype=jnp.int32)).astype(jnp.float32)
    slab_mask = lax.dynamic_slice_in_dim(mask_float, row_start, slab_rows)
    weighting = (
        (1.0 + (row_float[:, None] + col_float[None, :]) / total_len)
        * slab_mask[:, None]
        * col_mask[None, :]
    )
    update_float = update.astype(jnp.float32)
    partial_sum = jnp.sum(update_float * update_float * weighting[None])
    energy = lax.psum(partial_sum, ("gx", "gy", "gz")) / (total_len * total_len * channel_count)
    return (update, energy)


def solution(mesh):
    in_specs = (P("gx", "gy", None), P(), P(), P(None, None, "gz"), P(), P(), P())
    out_specs = (P(None, ("gx", "gz"), "gy"), P())
    return jax.shard_map(local, mesh=mesh, in_specs=in_specs, out_specs=out_specs, check_vma=False)
```

profile of v0, /device:TPU:12, one launch (start us, length us, event | category | flops | bytes accessed | tf_op | source)
XLA Modules:
  0.0 1946.3 jit_solution(17689445060744639698)
XLA Ops:
  7.2 0.8 convert_element_type.61
  8.1 11.7 convert_reduce_fusion
  19.8 19.0 fusion.2
  39.7 21.9 %fusion.4 = bf16[256,256,128]{2,1,0:T(8,128)(2,1)} fusion(bf16[256,256,128]{2,1,0:T(8,128)(2,1)} %param.7, f32[128]{0:T(128)S(1)} %copy-done.7, f32[256,256]{1,0:T(8,128)S(1)} %add_rsqrt_fusion, f32[256,256]{1,0:T(8,128)S(1)} %broadcast_multiply_fusion.1), kind=kLoop, calls=%fused_computation.6 | loop fusion | flops 41943040 | bytes 34079232 | tf_op jit(solution)/shard_map/convert_element_type | solution.py:34
  61.6 35.2 %convolution_bitcast_fusion = f32[4,64,256,256]{3,1,0,2:T(8,128)} fusion(bf16[256,256,128]{2,1,0:T(8,128)(2,1)} %fusion.4, bf16[128,4,64]{0,2,1:T(8,128)(2,1)S(1)} %copy-done), kind=kOutput, calls=%fused_computation.13 | convolution fusion | flops 4294967296 | bytes 83951616 | tf_op jit(solution)/shard_map/ijd,dkh->khij/dot_general | solution.py:35
  96.8 29.8 %fusion.12 = (bf16[64,256,256]{2,0,1:T(8,128)(2,1)}, bf16[64,256,256]{2,0,1:T(8,128)(2,1)}) fusion(f32[4,64,256,256]{3,1,0,2:T(8,128)} %convolution_bitcast_fusion, f32[256,256]{1,0:T(8,128)S(1)} %broadcast_multiply_fusion), kind=kLoop, calls=%fused_computation.16 | loop fusion | flops 50331648 | bytes 84148224 | tf_op jit(solution)/shard_map/convert_element_type | solution.py:37
  128.7 557.8 %all-gather.11.cloned.1.call-done = bf16[64,1024,256]{2,0,1:T(8,128)(2,1)} async-done(((bf16[64,256,256]{2,0,1:T(8,128)(2,1)}), bf16[64,1024,256]{2,0,1:T(8,128)(2,1)}) %all-gather.11.cloned.1.call-update) | async-done | bytes 33554448 | tf_op jit(solution)/shard_map/all_gather | solution.py:39
  686.6 209.1 %all-gather.9.cloned.1.call-done = bf16[64,256,1024]{2,0,1:T(8,128)(2,1)} async-done(((bf16[64,256,256]{2,0,1:T(8,128)(2,1)}), bf16[64,256,1024]{2,0,1:T(8,128)(2,1)}) %all-gather.9.cloned.1.call-update) | async-done | bytes 33554448 | tf_op jit(solution)/shard_map/all_gather | solution.py:43
  895.7 51.4 %fusion.5 = f32[64,256,256]{2,1,0:T(8,128)} fusion(bf16[64,1024,256]{2,0,1:T(8,128)(2,1)} %all-gather.11.cloned.1.call-done, bf16[64,256,1024]{2,0,1:T(8,128)(2,1)} %all-gather.9.cloned.1.call-done), kind=kOutput, calls=%fused_computation.7 | convolution fusion | flops 8589934592 | bytes 83886080 | tf_op jit(solution)/shard_map/hik,hkj->hij/dot_general | solution.py:17
  947.0 156.2 %all-gather.5.cloned.1.call-done = bf16[64,256,1024]{2,0,1:T(8,128)(2,1)} async-done(((bf16[64,256,256]{2,0,1:T(8,128)(2,1)}), bf16[64,256,1024]{2,0,1:T(8,128)(2,1)}) %all-gather.5.cloned.1.call-update) | async-done | bytes 33554448 | tf_op jit(solution)/shard_map/all_gather | solution.py:42
  1103.3 560.7 %all-gather.7.cloned.1.call-done = bf16[64,1024,256]{2,0,1:T(8,128)(2,1)} async-done(((bf16[64,256,256]{2,0,1:T(8,128)(2,1)}), bf16[64,1024,256]{2,0,1:T(8,128)(2,1)}) %all-gather.7.cloned.1.call-update) | async-done | bytes 33554448 | tf_op jit(solution)/shard_map/all_gather | solution.py:40
  1663.9 64.8 %multiply_convert_fusion.1 = bf16[64,256,256]{2,1,0:T(8,128)(2,1)} fusion(f32[64,256,256]{2,1,0:T(8,128)} %fusion.5, bf16[64,1024,256]{2,0,1:T(8,128)(2,1)} %all-gather.7.cloned.1.call-done, bf16[64,256,1024]{2,0,1:T(8,128)(2,1)} %all-gather.5.cloned.1.call-done), kind=kOutput, calls=%fused_computation.43 | convolution fusion | flops 8602517504 | bytes 92274688 | tf_op jit(solution)/shard_map/hik,hkj->hij/dot_general | solution.py:17
  1728.7 11.4 copy.45
  1740.1 7.4 all-to-all-start
  1748.4 11.5 fusion.37
  1759.9 78.6 %all-to-all-done = bf16[64,256,256]{2,0,1:T(8,128)(2,1)} async-done(((bf16[64,256,256]{2,0,1:T(8,128)(2,1)}), bf16[64,256,256]{2,0,1:T(8,128)(2,1)}, u32[]{:S(2)}, u32[]{:S(2)}) %all-to-all-start) | async-done | bytes 8388640 | tf_op jit(solution)/shard_map/all_to_all | solution.py:50
  1838.5 11.5 fusion.46
  1850.0 1.2 fusion.35
  1851.2 2.2 multiply_reduce_fusion.1
  1853.5 7.7 copy.47
  1861.2 5.6 fusion.30
  1866.9 14.6 multiply_reduce_fusion
  1881.4 12.7 copy.49
  1894.2 43.7 %psum.7 = f32[]{:T(128)} all-reduce(f32[]{:T(128)} %get-tuple-element.16), channel_id=1, replica_groups=mesh['gx'=4,'gy'=4,'gz'=2] {'gx','gy','gz'}, use_global_device_ids=true, to_apply=%region_5.0 | all-reduce | flops 1 | bytes 8 | tf_op jit(solution)/shard_map/psum | solution.py:71
  (47 shorter events, 3.9 us)
Async XLA Ops:
  7.2 54.5 %copy-start = (bf16[128,4,64]{0,2,1:T(8,128)(2,1)S(1)}, bf16[128,4,64]{0,2,1:T(8,128)(2,1)}, u32[]{:S(2)}) copy-start(bf16[128,4,64]{0,2,1:T(8,128)(2,1)} %param.10) | copy-start | bytes 196612
  7.2 679.4 %all-gather.11.cloned.1.call-start = ((), (), s32[]{:S(2)}) async-start(), calls=%async_computation.4 | async-start | bytes 41943040 | tf_op jit(solution)/shard_map/all_gather | solution.py:39
  7.2 12.6 copy-start.2
  8.1 30.8 %copy-start.6 = (f32[1024]{0:T(1024)}, f32[1024]{0:T(1024)S(1)}, u32[]{:S(2)}) copy-start(f32[1024]{0:T(1024)S(1)} %convert_element_type.61) | copy-start | bytes 12292
  8.1 31.6 %copy-start.7 = (f32[128]{0:T(128)S(1)}, f32[128]{0:T(128)}, u32[]{:S(2)}) copy-start(f32[128]{0:T(128)} %param.9) | copy-start | bytes 1540
  39.0 0.6 copy-start.4
  126.7 769.0 %all-gather.9.cloned.1.call-start = ((), (), s32[]{:S(2)}) async-start(), calls=%async_computation.3 | async-start | bytes 41943040 | tf_op jit(solution)/shard_map/all_gather | solution.py:43
  127.4 975.8 %all-gather.5.cloned.1.call-start = ((), (), s32[]{:S(2)}) async-start(), calls=%async_computation.1 | async-start | bytes 41943040 | tf_op jit(solution)/shard_map/all_gather | solution.py:42
  128.2 1535.8 %all-gather.7.cloned.1.call-start = ((), (), s32[]{:S(2)}) async-start(), calls=%async_computation.2 | async-start | bytes 41943040 | tf_op jit(solution)/shard_map/all_gather | solution.py:40
  1728.7 19.6 %copy-start.5 = (f32[256]{0:T(256)S(1)}, f32[256]{0:T(256)}, u32[]{:S(2)}) copy-start(f32[256]{0:T(256)} %copy-done.4) | copy-start | bytes 3076
  1728.7 19.7 %copy-start.3 = (bf16[128,128]{1,0:T(8,128)(2,1)S(1)}, bf16[128,128]{1,0:T(8,128)(2,1)}, u32[]{:S(2)}) copy-start(bf16[128,128]{1,0:T(8,128)(2,1)} %param.11) | copy-start | bytes 98308
  1740.1 98.3 %all-to-all-start = ((bf16[64,256,256]{2,0,1:T(8,128)(2,1)}), bf16[64,256,256]{2,0,1:T(8,128)(2,1)}, u32[]{:S(2)}, u32[]{:S(2)}) async-start(bf16[64,256,256]{2,0,1:T(8,128)(2,1)} %copy.45), calls=%async_computation | async-start | bytes 16777216 | tf_op jit(solution)/shard_map/all_to_all | solution.py:50
  1853.4 7.8 copy-start.8
  1853.4 13.4 slice-start
  1853.5 13.4 slice-start.1
  1853.5 13.4 slice-start.2
  1861.2 5.6 slice-start.3
  1861.2 5.6 copy-start.9
  1866.9 71.6 %copy-start.1 = (bf16[128,4,64]{0,2,1:T(8,128)(2,1)S(1)}, bf16[128,4,64]{0,2,1:T(8,128)(2,1)}, u32[]{:S(2)}) copy-start(bf16[128,4,64]{0,2,1:T(8,128)(2,1)} %param.10) | copy-start | bytes 196612
Sparse Core Ops, SparseCore 0:
  126.8 559.7 all-gather.10
  688.7 206.9 all-gather.8
  897.2 205.9 all-gather.4
  1105.2 558.6 all-gather.6
where the time goes:
time: 1950 us
  waiting for transfers between devices  1560 us (80%)
  matrix products  177 us (9%)
  other arithmetic  104 us (5%)
  blocking collectives  43.7 us (2%)
  local copies, waits for them, and re-layouts  33.3 us (2%)
    all_gather x1, waiting for transfers between devices, local(): lax.all_gather(right_tile, 'gx', axis=1, tiled=True)  561 us
    all_gather x1, waiting for transfers between devices, local(): lax.all_gather(left_tile, 'gx', axis=1, tiled=True)  558 us
    all_gather x1, waiting for transfers between devices, local(): piece_right = lax.all_gather(right_tile, 'gy', axis=2, tiled=True)  209 us
    all_gather x1, waiting for transfers between devices, local(): piece_left = lax.all_gather(left_tile, 'gy', axis=2, tiled=True)  156 us
    dot_general x2, matrix products, batched(): jnp.einsum('hik,hkj->hij', first, second, preferred_element_type=jnp.floa...  116 us
    all_to_all x1, waiting for transfers between devices, local(): lax.all_to_all(tri_map, 'gz', split_axis=1, concat_axis=0, tiled=True)  78.6 us
    psum x1, blocking collectives, local(): lax.psum(partial_sum, ('gx', 'gy', 'gz'))  43.7 us
  transfers between devices with their start and end apart: 5, of which 5 were waited for; matrix products, arithmetic and copies ran while one was open for 3% of the time, Pallas kernels for 0%

commit v1 on v0

--- a/solution.py
+++ b/solution.py
@@ -39,7 +39,12 @@
         lax.all_gather(left_tile, "gx", axis=1, tiled=True),
         lax.all_gather(right_tile, "gx", axis=1, tiled=True),
     )
-    piece_left = lax.all_gather(left_tile, "gy", axis=2, tiled=True)
+    ring = [left_tile]
+    for hop in range(3):
+        ring.append(lax.ppermute(ring[-1], "gy", [(dev, (dev + 1) % 4) for dev in range(4)]))
+    piece_left = jnp.roll(
+        jnp.concatenate(ring[::-1], axis=2), (lax.axis_index("gy") + 1) * ring[0].shape[2], axis=2
+    )
     piece_right = lax.all_gather(right_tile, "gy", axis=2, tiled=True)
     below_left = col_left
     below_right = col_right

time: 1950 us -> 1750 us (0.90)
  waiting for transfers between devices: 1560 us -> 1260 us
  local copies, waits for them, and re-layouts: 33.3 us -> 128 us
    all_gather x1, waiting for transfers between devices: 558 us -> 185 us  [local(): lax.all_gather(left_tile, 'gx', axis=1, tiled=True)]
    ppermute x0 -> x3, waiting for transfers between devices: none -> 279 us  [local(): lax.ppermute(ring[-1], 'gy', [(dev, (dev + 1) % 4) for dev in range(4)])]
    all_gather x1 -> x0, waiting for transfers between devices: 156 us -> none  [local(): piece_left = lax.all_gather(left_tile, 'gy', axis=2, tiled=True)]
    unnamed x29 -> x38, local copies, waits for them, and re-layouts: 13.4 us -> 76 us
    all_gather x1, waiting for transfers between devices: 561 us -> 509 us  [local(): lax.all_gather(right_tile, 'gx', axis=1, tiled=True)]
    dynamic_slice x0 -> x1, local copies, waits for them, and re-layouts: none -> 23.3 us  [local(): jnp.roll(jnp.concatenate(ring[::-1], axis=2), (lax.axis_index('gy') + 1)...]
  transfers between devices with their start and end apart: 5 -> 7, of which waited for: 5 -> 7; matrix products, arithmetic and copies ran while one was open for 3% -> 9% of each run, Pallas kernels for 0% -> 0%
where the time goes in v1:
time: 1750 us; the launch traced here: 1740 us
  waiting for transfers between devices  1260 us (72%)
  matrix products  178 us (10%)
  local copies, waits for them, and re-layouts  128 us (7%)
  other arithmetic  104 us (6%)
  blocking collectives  43.7 us (2%)
    all_gather x1, waiting for transfers between devices, local(): lax.all_gather(right_tile, 'gx', axis=1, tiled=True)  509 us
    ppermute x3, waiting for transfers between devices, local(): lax.ppermute(ring[-1], 'gy', [(dev, (dev + 1) % 4) for dev in range(4)])  279 us
    all_gather x1, waiting for transfers between devices, local(): piece_right = lax.all_gather(right_tile, 'gy', axis=2, tiled=True)  209 us
    all_gather x1, waiting for transfers between devices, local(): lax.all_gather(left_tile, 'gx', axis=1, tiled=True)  185 us
    dot_general x2, matrix products, batched(): jnp.einsum('hik,hkj->hij', first, second, preferred_element_type=jnp.floa...  116 us
    all_to_all x1, waiting for transfers between devices, local(): lax.all_to_all(tri_map, 'gz', split_axis=1, concat_axis=0, tiled=True)  78.6 us
    unnamed x38, local copies, waits for them, and re-layouts  76 us
    psum x1, blocking collectives, local(): lax.psum(partial_sum, ('gx', 'gy', 'gz'))  43.7 us
  transfers between devices with their start and end apart: 7, of which 7 were waited for; matrix products, arithmetic and copies ran while one was open for 9% of the time, Pallas kernels for 0%

profile of v1, /device:TPU:12, one launch (start us, length us, event | category | flops | bytes accessed | tf_op | source)
XLA Modules:
  0.0 1738.8 jit_solution(7913512375947977390)
XLA Ops:
  8.1 11.7 convert_reduce_fusion
  19.8 19.0 %fusion.2 = f32[256,256]{1,0:T(8,128)S(1)} fusion(bf16[256,256,128]{2,1,0:T(8,128)(2,1)S(1)} %copy-done.2, f32[256,256]{1,0:T(8,128)S(1)} %broadcast_multiply_fusion.1), kind=kLoop, calls=%fused_computation.4 | loop fusion | flops 33488896 | bytes 17301504 | tf_op jit(solution)/shard_map/reduce_sum | solution.py:12
  39.7 21.9 %fusion.4 = bf16[256,256,128]{2,1,0:T(8,128)(2,1)} fusion(bf16[256,256,128]{2,1,0:T(8,128)(2,1)} %param.7, f32[128]{0:T(128)S(1)} %copy-done.8, f32[256,256]{1,0:T(8,128)S(1)} %add_rsqrt_fusion, f32[256,256]{1,0:T(8,128)S(1)} %broadcast_multiply_fusion.1), kind=kLoop, calls=%fused_computation.6 | loop fusion | flops 41943040 | bytes 34079232 | tf_op jit(solution)/shard_map/convert_element_type | solution.py:34
  61.6 35.3 %convolution_bitcast_fusion = f32[4,64,256,256]{3,1,0,2:T(8,128)} fusion(bf16[256,256,128]{2,1,0:T(8,128)(2,1)} %fusion.4, bf16[128,4,64]{0,2,1:T(8,128)(2,1)S(1)} %copy-done), kind=kOutput, calls=%fused_computation.13 | convolution fusion | flops 4294967296 | bytes 83951616 | tf_op jit(solution)/shard_map/ijd,dkh->khij/dot_general | solution.py:35
  96.9 29.8 %fusion.12 = (bf16[64,256,256]{2,0,1:T(8,128)(2,1)}, bf16[64,256,256]{2,0,1:T(8,128)(2,1)}) fusion(f32[4,64,256,256]{3,1,0,2:T(8,128)} %convolution_bitcast_fusion, f32[256,256]{1,0:T(8,128)S(1)} %broadcast_multiply_fusion), kind=kLoop, calls=%fused_computation.16 | loop fusion | flops 50331648 | bytes 84148224 | tf_op jit(solution)/shard_map/convert_element_type | solution.py:37
  128.3 93.1 %collective-permute-done = bf16[64,256,256]{2,0,1:T(8,128)(2,1)S(1)} collective-permute-done((bf16[64,256,256]{2,0,1:T(8,128)(2,1)}, bf16[64,256,256]{2,0,1:T(8,128)(2,1)S(1)}, u32[]{:S(2)}, u32[]{:S(2)}) %collective-permute-start) | collective-permute-done | bytes 8388640 | tf_op jit(solution)/shard_map/ppermute | solution.py:44
  224.6 93.0 %collective-permute-done.1 = bf16[64,256,256]{2,0,1:T(8,128)(2,1)} collective-permute-done((bf16[64,256,256]{2,0,1:T(8,128)(2,1)S(1)}, bf16[64,256,256]{2,0,1:T(8,128)(2,1)}, u32[]{:S(2)}, u32[]{:S(2)}) %collective-permute-start.1) | collective-permute-done | bytes 8388640 | tf_op jit(solution)/shard_map/ppermute | solution.py:44
  317.7 93.2 %collective-permute-done.2 = bf16[64,256,256]{2,0,1:T(8,128)(2,1)} collective-permute-done((bf16[64,256,256]{2,0,1:T(8,128)(2,1)}, bf16[64,256,256]{2,0,1:T(8,128)(2,1)}, u32[]{:S(2)}, u32[]{:S(2)}) %collective-permute-start.2) | collective-permute-done | bytes 8388640 | tf_op jit(solution)/shard_map/ppermute | solution.py:44
  419.3 8.6 constant_dynamic-update-slice_fusion.6
  444.8 8.5 constant_dynamic-update-slice_fusion.3
  461.7 8.6 constant_dynamic-update-slice_fusion.1
  478.7 23.3 %constant_dynamic-slice_fusion = bf16[64,256,1024]{2,0,1:T(8,128)(2,1)} fusion(bf16[64,256,2048]{2,0,1:T(8,128)(2,1)} %constant_dynamic-update-slice_fusion, s32[]{:T(128)S(6)} %select_n.29), kind=kLoop, calls=%fused_computation.68 | loop fusion | bytes 67108864 | tf_op jit(solution)/shard_map/jit(_roll_dynamic)/dynamic_slice | solution.py:45
  502.1 184.5 %all-gather.8.cloned.1.call-done = bf16[64,1024,256]{2,0,1:T(8,128)(2,1)} async-done(((bf16[64,256,256]{2,0,1:T(8,128)(2,1)}), bf16[64,1024,256]{2,0,1:T(8,128)(2,1)}) %all-gather.8.cloned.1.call-update) | async-done | bytes 33554448 | tf_op jit(solution)/shard_map/all_gather | solution.py:39
  686.6 209.1 %all-gather.6.cloned.1.call-done = bf16[64,256,1024]{2,0,1:T(8,128)(2,1)} async-done(((bf16[64,256,256]{2,0,1:T(8,128)(2,1)}), bf16[64,256,1024]{2,0,1:T(8,128)(2,1)}) %all-gather.6.cloned.1.call-update) | async-done | bytes 33554448 | tf_op jit(solution)/shard_map/all_gather | solution.py:48
  895.7 51.4 %fusion.5 = f32[64,256,256]{2,1,0:T(8,128)} fusion(bf16[64,1024,256]{2,0,1:T(8,128)(2,1)} %all-gather.8.cloned.1.call-done, bf16[64,256,1024]{2,0,1:T(8,128)(2,1)} %all-gather.6.cloned.1.call-done), kind=kOutput, calls=%fused_computation.7 | convolution fusion | flops 8589934592 | bytes 83886080 | tf_op jit(solution)/shard_map/hik,hkj->hij/dot_general | solution.py:17
  947.1 509.4 %all-gather.4.cloned.1.call-done = bf16[64,1024,256]{2,0,1:T(8,128)(2,1)} async-done(((bf16[64,256,256]{2,0,1:T(8,128)(2,1)}), bf16[64,1024,256]{2,0,1:T(8,128)(2,1)}) %all-gather.4.cloned.1.call-update) | async-done | bytes 33554448 | tf_op jit(solution)/shard_map/all_gather | solution.py:40
  1456.5 65.0 %multiply_convert_fusion.1 = bf16[64,256,256]{2,1,0:T(8,128)(2,1)} fusion(f32[64,256,256]{2,1,0:T(8,128)} %fusion.5, bf16[64,1024,256]{2,0,1:T(8,128)(2,1)} %all-gather.4.cloned.1.call-done, bf16[64,256,1024]{2,0,1:T(8,128)(2,1)} %constant_dynamic-slice_fusion), kind=kOutput, calls=%fused_computation.43 | convolution fusion | flops 8602517504 | bytes 92274688 | tf_op jit(solution)/shard_map/hik,hkj->hij/dot_general | solution.py:17
  1521.6 11.4 copy.45
  1541.3 11.5 fusion.37
  1552.7 78.6 %all-to-all-done = bf16[64,256,256]{2,0,1:T(8,128)(2,1)} async-done(((bf16[64,256,256]{2,0,1:T(8,128)(2,1)}), bf16[64,256,256]{2,0,1:T(8,128)(2,1)}, u32[]{:S(2)}, u32[]{:S(2)}) %all-to-all-start) | async-done | bytes 8388640 | tf_op jit(solution)/shard_map/all_to_all | solution.py:55
  1631.3 11.2 fusion.46
  1659.4 14.5 multiply_reduce_fusion
  1673.9 12.7 copy.49
  1686.7 43.7 %psum.7 = f32[]{:T(128)} all-reduce(f32[]{:T(128)} %get-tuple-element.16), channel_id=1, replica_groups=mesh['gx'=4,'gy'=4,'gz'=2] {'gx','gy','gz'}, use_global_device_ids=true, to_apply=%region_5.6 | all-reduce | flops 1 | bytes 8 | tf_op jit(solution)/shard_map/psum | solution.py:76
  (61 shorter events, 73.9 us)
Async XLA Ops:
  7.2 54.5 %copy-start = (bf16[128,4,64]{0,2,1:T(8,128)(2,1)S(1)}, bf16[128,4,64]{0,2,1:T(8,128)(2,1)}, u32[]{:S(2)}) copy-start(bf16[128,4,64]{0,2,1:T(8,128)(2,1)} %param.10) | copy-start | bytes 196612
  7.2 679.4 %all-gather.8.cloned.1.call-start = ((), (), s32[]{:S(2)}) async-start(), calls=%async_computation.3 | async-start | bytes 41943040 | tf_op jit(solution)/shard_map/all_gather | solution.py:39
  7.2 12.6 copy-start.2
  8.1 30.8 %copy-start.7 = (f32[1024]{0:T(1024)}, f32[1024]{0:T(1024)S(1)}, u32[]{:S(2)}) copy-start(f32[1024]{0:T(1024)S(1)} %convert_element_type.61) | copy-start | bytes 12292
  8.1 31.6 %copy-start.8 = (f32[128]{0:T(128)S(1)}, f32[128]{0:T(128)}, u32[]{:S(2)}) copy-start(f32[128]{0:T(128)} %param.9) | copy-start | bytes 1540
  39.0 0.6 copy-start.5
  126.7 769.0 %all-gather.6.cloned.1.call-start = ((), (), s32[]{:S(2)}) async-start(), calls=%async_computation.2 | async-start | bytes 41943040 | tf_op jit(solution)/shard_map/all_gather | solution.py:48
  127.5 1329.1 %all-gather.4.cloned.1.call-start = ((), (), s32[]{:S(2)}) async-start(), calls=%async_computation.1 | async-start | bytes 41943040 | tf_op jit(solution)/shard_map/all_gather | solution.py:40
  128.2 93.1 %collective-permute-start = (bf16[64,256,256]{2,0,1:T(8,128)(2,1)}, bf16[64,256,256]{2,0,1:T(8,128)(2,1)S(1)}, u32[]{:S(2)}, u32[]{:S(2)}) collective-permute-start(bf16[64,256,256]{2,0,1:T(8,128)(2,1)} %get-tuple-element.11), channel_id=1, source_target_pairs={{0,2},{2,4},{4,6},{6,0},{1,3},{3,5},{5,7},{7,1},{8,10},{10,12},{12... | collective-permute-start | bytes 25165832 | tf_op jit(solution)/shard_map/ppermute | solution.py:44
  221.3 3.2 copy-start.3
  224.6 93.0 %collective-permute-start.1 = (bf16[64,256,256]{2,0,1:T(8,128)(2,1)S(1)}, bf16[64,256,256]{2,0,1:T(8,128)(2,1)}, u32[]{:S(2)}, u32[]{:S(2)}) collective-permute-start(bf16[64,256,256]{2,0,1:T(8,128)(2,1)S(1)} %collective-permute-done), channel_id=1, source_target_pairs={{0,2},{2,4},{4,6},{6,0},{1,3},{3,5},{5,7},{7,1},{8,10},{10,12},{12... | collective-permute-start | bytes 25165832 | tf_op jit(solution)/shard_map/ppermute | solution.py:44
  317.5 93.3 %collective-permute-start.2 = (bf16[64,256,256]{2,0,1:T(8,128)(2,1)}, bf16[64,256,256]{2,0,1:T(8,128)(2,1)}, u32[]{:S(2)}, u32[]{:S(2)}) collective-permute-start(bf16[64,256,256]{2,0,1:T(8,128)(2,1)} %collective-permute-done.1), channel_id=1, source_target_pairs={{0,2},{2,4},{4,6},{6,0},{1,3},{3,5},{5,7},{7,1},{8,10},{10,12},{12... | collective-permute-start | bytes 25165832 | tf_op jit(solution)/shard_map/ppermute | solution.py:44
  1521.6 19.6 %copy-start.6 = (f32[256]{0:T(256)S(1)}, f32[256]{0:T(256)}, u32[]{:S(2)}) copy-start(f32[256]{0:T(256)} %copy-done.5) | copy-start | bytes 3076
  1521.6 19.7 %copy-start.4 = (bf16[128,128]{1,0:T(8,128)(2,1)S(1)}, bf16[128,128]{1,0:T(8,128)(2,1)}, u32[]{:S(2)}) copy-start(bf16[128,128]{1,0:T(8,128)(2,1)} %param.11) | copy-start | bytes 98308
  1533.0 98.3 %all-to-all-start = ((bf16[64,256,256]{2,0,1:T(8,128)(2,1)}), bf16[64,256,256]{2,0,1:T(8,128)(2,1)}, u32[]{:S(2)}, u32[]{:S(2)}) async-start(bf16[64,256,256]{2,0,1:T(8,128)(2,1)} %copy.45), calls=%async_computation | async-start | bytes 16777216 | tf_op jit(solution)/shard_map/all_to_all | solution.py:55
  1646.0 7.8 copy-start.9
  1646.0 13.4 slice-start
  1646.0 13.4 slice-start.1
  1646.0 13.4 slice-start.2
  1653.8 5.6 slice-start.3
  1653.8 5.6 copy-start.10
  1659.4 71.5 %copy-start.1 = (bf16[128,4,64]{0,2,1:T(8,128)(2,1)S(1)}, bf16[128,4,64]{0,2,1:T(8,128)(2,1)}, u32[]{:S(2)}) copy-start(bf16[128,4,64]{0,2,1:T(8,128)(2,1)} %param.10) | copy-start | bytes 196612
Sparse Core Ops, SparseCore 0:
  126.8 559.7 all-gather.7
  688.7 206.9 all-gather.5
  897.9 558.6 all-gather.3
